TPU v7x, 32 devices: a whole 2x2x4 slice. The times are simulated.
32 devices in a mesh: gx: 4 (over y, x), gy: 4 (over z), row: 2 (over core).
Axes of the slice: x: 2, y: 2, z: 4, core: 2. Of those that a mesh axis runs over, the one named last changes fastest.
Arguments:
- columns: bfloat16 [137, 131072], P(None, ('gx', 'gy')), may hold values from -6 to 6
- level_weights: bfloat16 [137, 16], replicated, may hold values from -0.5 to 0.5
- orbit_term: float32 [16, 32], replicated, may hold values from -6 to 6
- col_owner: int32 [524288, 1], P(('gx', 'gy', 'row')), may hold values from 0 to 15; in each aligned block of 16384 rows (0 to 16383, 16384 to 32767, ...) at most 2048 rows name the same one
- col_local: int32 [524288], P(('gx', 'gy', 'row')), may hold values from 0 to 8191
- orbit_bin: int32 [524288], P(('gx', 'gy', 'row')), may hold values from 0 to 31
- group_id: int32 [524288], P(('gx', 'gy', 'row')), may hold values from 0 to 63
- departure: float32 [524288], P(('gx', 'gy', 'row')), may hold values from -6 to 6
Outputs:
- covariance: float32 [16, 16, 64], P(None, None, 'row')
- cross: float32 [16, 64], P(None, 'row')
Inputs may be any that keep to these rules, and one draw needn't show every extreme that they name: `col_owner`: among the footprints of one device, no owning device is named more than 2048 times; some owning device is named exactly 2048 times.
All inputs are finite; a program needn't handle non-finite values.
Results may differ from a plain program's by a relative error of at most 0.0022.
Values may be sent and summed in bfloat16 or wider, within the bound.
A program may use at most 128 MiB of HBM per device.

v0:
```python
import math

import jax
import jax.numpy as jnp
from jax import lax
from jax.sharding import PartitionSpec as P

NGRP = 64


def send_request(wanted):
    return lax.all_to_all(wanted, ("gx", "gy"), split_axis=0, concat_axis=0, tiled=True)


def send_answer(picked):
    return lax.all_to_all(picked, ("gx", "gy"), split_axis=1, concat_axis=1, tiled=True)


def local(columns, level_weights, orbit_term, col_owner, col_local, orbit_bin, group_id, departure):
    grid_x = lax.axis_size("gx")
    grid_y = lax.axis_size("gy")
    owners = grid_x * grid_y
    footprints = col_owner.shape[0]
    capacity = 2 * footprints // owners
    slots_all = owners * capacity
    npred = level_weights.shape[1]
    ngroups = NGRP
    owner = col_owner[:, 0]
    owner_hits = (owner[:, None] == jnp.arange(owners, dtype=jnp.int32)[None, :]).astype(jnp.int32)
    ranks = jnp.cumsum(owner_hits, axis=0)
    slot = jnp.sum(ranks * owner_hits, axis=1) - 1
    target = owner * capacity + slot
    stacked = jnp.stack([col_local, orbit_bin, group_id], axis=0)
    placed = jnp.full((3, slots_all), -1, jnp.int32).at[:, target].set(stacked)
    slot_depart = jnp.zeros((slots_all,), jnp.float32).at[target].set(departure)
    wanted = jnp.maximum(placed[0], 0).reshape(owners, capacity)
    asked = send_request(wanted)
    thickness = jnp.dot(level_weights.T, columns, preferred_element_type=jnp.float32).astype(
        jnp.bfloat16
    )
    picked = thickness[:, asked]
    back = send_answer(picked)
    flat = back.reshape(npred, slots_all)
    slot_bin = placed[1]
    slot_group = placed[2]
    width = math.gcd(slots_all, 4096)
    nblocks = slots_all // width
    bin_range = jnp.arange(orbit_term.shape[1], dtype=jnp.int32)
    group_range = jnp.arange(ngroups, dtype=jnp.int32)

    def accumulate(carry, which):
        prod_acc, sum_acc, count_acc = carry
        first = which * width
        part_flat = lax.dynamic_slice_in_dim(flat, first, width, 1)
        part_bin = lax.dynamic_slice_in_dim(slot_bin, first, width, 0)
        grp = lax.dynamic_slice_in_dim(slot_group, first, width, 0)
        dep = lax.dynamic_slice_in_dim(slot_depart, first, width, 0)
        bin_hits = (bin_range[:, None] == part_bin[None, :]).astype(jnp.float32)
        block = part_flat.astype(jnp.float32) + jnp.dot(
            orbit_term,
            bin_hits,
            precision=lax.Precision.HIGHEST,
            preferred_element_type=jnp.float32,
        )
        hits = (grp[:, None] == group_range[None, :]).astype(jnp.float32)
        outer = (block[:, None, :] * block[None, :, :]).reshape(npred * npred, width)
        prod_acc = prod_acc + jnp.dot(
            outer, hits, precision=lax.Precision.HIGHEST, preferred_element_type=jnp.float32
        )
        sum_acc = sum_acc + jnp.dot(
            block * dep[None, :],
            hits,
            precision=lax.Precision.HIGHEST,
            preferred_element_type=jnp.float32,
        )
        count_acc = count_acc + jnp.sum(hits, axis=0)[None, :]
        return ((prod_acc, sum_acc, count_acc), None)

    start = (
        jnp.zeros((npred * npred, ngroups), jnp.float32),
        jnp.zeros((npred, ngroups), jnp.float32),
        jnp.zeros((1, ngroups), jnp.float32),
    )
    (products, sums, count), _ = lax.scan(accumulate, start, jnp.arange(nblocks, dtype=jnp.int32))
    share = ngroups // lax.axis_size("row")
    products, sums, count = (
        lax.psum_scatter(products, "row", scatter_dimension=1, tiled=True),
        lax.psum_scatter(sums, "row", scatter_dimension=1, tiled=True),
        lax.psum_scatter(count, "row", scatter_dimension=1, tiled=True),
    )
    products, sums, count = lax.psum((products, sums, count), ("gx", "gy"))
    scale = 1.0 / (count + 1.0)
    covariance = (products * scale).reshape(npred, npred, share)
    cross = sums * scale
    return (covariance, cross)


def solution(mesh):
    in_specs = (
        P(None, ("gx", "gy")),
        P(),
        P(),
        P(("gx", "gy", "row"), None),
        P(("gx", "gy", "row")),
        P(("gx", "gy", "row")),
        P(("gx", "gy", "row")),
        P(("gx", "gy", "row")),
    )
    out_specs = (P(None, None, "row"), P(None, "row"))
    return jax.shard_map(local, mesh=mesh, in_specs=in_specs, out_specs=out_specs, check_vma=False)
```

profile of v0, /device:TPU:0, one launch (start us, length us, event | category | flops | bytes accessed | tf_op | source)
XLA Modules:
  0.0 520.1 jit_solution(6604722221456737863)
XLA Ops:
  11.4 1.6 fusion.17
  15.1 5.1 copy.37
  20.1 47.4 %scatter_custom_fusion = s32[3,32768]{0,1:T(8,128)} fusion(s32[16384]{0:T(1024)S(1)} %bitcast.78, s32[16384,3]{1,0:T(8,128)} %copy.37, s32[]{:T(128)} %constant.6.clone.1), kind=kCustom, calls=%fused_computation.26 | custom fusion | bytes 393728 | tf_op jit(solution)/shard_map/scatter | solution.py:34
  67.5 30.9 %slice_reduce_fusion = (s32[32768]{0:T(1024)}, s32[32768]{0:T(1024)}, s32[32768]{0:T(1024)}) fusion(s32[3,32768]{0,1:T(8,128)} %scatter_custom_fusion), kind=kLoop, calls=%fused_computation.21 | loop fusion | flops 32768 | bytes 786432 | tf_op jit(solution)/shard_map/slice | solution.py:45
  98.4 8.3 %all-to-all-start = ((s32[16,1,2048]{2,1,0:T(1,128)}), s32[16,1,2048]{2,1,0:T(1,128)S(1)}, u32[]{:S(2)}, u32[]{:S(2)}) async-start(s32[16,1,2048]{2,1,0:T(1,128)} %bitcast.24), calls=%async_computation | async-start | bytes 262144 | tf_op jit(solution)/shard_map/all_to_all | solution.py:12
  107.2 1.8 copy.39
  109.0 5.5 %all-to-all-done = s32[16,1,2048]{2,1,0:T(1,128)S(1)} async-done(((s32[16,1,2048]{2,1,0:T(1,128)}), s32[16,1,2048]{2,1,0:T(1,128)S(1)}, u32[]{:S(2)}, u32[]{:S(2)}) %all-to-all-start) | async-done | bytes 131104 | tf_op jit(solution)/shard_map/all_to_all | solution.py:12
  114.6 111.2 %gather_fusion = bf16[32768,16]{1,0:T(8,128)(2,1)} fusion(bf16[16,8192]{0,1:T(8,128)(2,1)} %copy.39, s32[32768]{0:T(1024)S(1)} %broadcast_clamp_fusion), kind=kCustom, calls=%fused_computation | custom fusion | bytes 2228224 | tf_op jit(solution)/shard_map/gather | solution.py:41
  225.8 7.8 %copy.40 = bf16[16,2048,16]{1,2,0:T(8,128)(2,1)} copy(bf16[16,2048,16]{2,1,0:T(8,128)(2,1)} %bitcast.64) | data formatting | bytes 2097152 | tf_op jit(solution)/shard_map/gather | solution.py:41
  233.6 3.7 all-to-all-start.1
  237.4 61.1 %scatter_custom_fusion.1 = f32[32768]{0:T(1024)} fusion(s32[16384]{0:T(1024)S(1)} %bitcast.79, f32[16384]{0:T(1024)} %param.17, f32[]{:T(128)} %constant.20.clone.1), kind=kCustom, calls=%fused_computation.41 | custom fusion | bytes 131584 | tf_op jit(solution)/shard_map/scatter | solution.py:35
  299.6 103.2 %while.15 = (s32[]{:T(128)}, f32[256,64]{0,1:T(8,128)S(1)}, f32[16,64]{1,0:T(8,128)}, f32[1,64]{1,0:T(1,128)S(1)}, s32[8]{0:T(128)S(1)}, /*index=5*/bf16[16,3276...) while((s32[]{:T(128)}, f32[256,64]{0,1:T(8,128)S(1)}, ...), condition=%wide.region_7.8_spmd.clone, body=%wide.region_5.7_spmd.clone.sunk | while | flops 883525696 | bytes 9661715 | solution.py:84
  302.9 2.4 broadcast_multiply_fusion.4
  306.0 4.5 convolution_add_fusion.4
  315.8 2.4 broadcast_multiply_fusion.4
  318.9 4.5 convolution_add_fusion.4
  328.7 2.4 broadcast_multiply_fusion.4
  331.8 4.5 convolution_add_fusion.4
  341.6 2.4 broadcast_multiply_fusion.4
  344.7 4.5 convolution_add_fusion.4
  354.5 2.4 broadcast_multiply_fusion.4
  357.6 4.5 convolution_add_fusion.4
  367.4 2.4 broadcast_multiply_fusion.4
  370.5 4.5 convolution_add_fusion.4
  380.3 2.4 broadcast_multiply_fusion.4
  383.4 4.5 convolution_add_fusion.4
  393.2 2.4 broadcast_multiply_fusion.4
  396.3 4.5 convolution_add_fusion.4
  405.7 6.7 %reduce-scatter.10.cloned.1.call-done = f32[32,1]{1,0:T(8,128)} async-done(((f32[64,1]{1,0:T(8,128)}), f32[32,1]{1,0:T(8,128)}) %reduce-scatter.10.cloned.1.call-update) | async-done | bytes 144
  413.2 10.1 %reduce-scatter.12.cloned.1.call-done = f32[32,16]{1,0:T(8,128)} async-done(((f32[64,16]{1,0:T(8,128)}), f32[32,16]{1,0:T(8,128)}) %reduce-scatter.12.cloned.1.call-update) | async-done | bytes 2064
  424.1 10.7 %reduce-scatter.8.cloned.1.call-done = f32[256,32]{0,1:T(8,128)} async-done(((f32[256,64]{0,1:T(8,128)}), f32[256,32]{0,1:T(8,128)}) %reduce-scatter.8.cloned.1.call-update) | async-done | bytes 32784 | tf_op jit(solution)/shard_map/reduce_scatter | solution.py:87
  434.8 77.4 %all-reduce = (f32[256,32]{0,1:T(8,128)S(1)}, f32[1,32]{1,0:T(1,128)S(1)}, f32[16,32]{1,0:T(8,128)S(1)}) all-reduce(f32[256,32]{0,1:T(8,128)} %reduce-scatter.8.cloned.1.call-done, f32[1,32]{1,0:T(1,128)S(1)} %copy.44, f32[16,32]{1,0:T(8,128)S(1)} %copy.46), channel_id=1, replica_groups=mesh['gx'=4,'gy'=4,'row'=2] {'gx','gy'}, use_global_device_ids=true, to_apply=%region_9.10 | all-reduce | flops 8736 | bytes 69888 | tf_op jit(solution)/shard_map/psum | solution.py:91
  (137 shorter events, 55.8 us)
Async XLA Ops:
  7.2 99.6 %copy-start = (bf16[137,8192]{1,0:T(8,128)(2,1)S(1)}, bf16[137,8192]{1,0:T(8,128)(2,1)}, u32[]{:S(2)}) copy-start(bf16[137,8192]{1,0:T(8,128)(2,1)} %param.10) | copy-start | bytes 6733828
  67.5 39.3 %copy-start.3 = (bf16[137,16]{0,1:T(8,128)(2,1)S(1)}, bf16[137,16]{0,1:T(8,128)(2,1)}, u32[]{:S(2)}) copy-start(bf16[137,16]{0,1:T(8,128)(2,1)} %param.11) | copy-start | bytes 13156
  98.4 16.0 %all-to-all-start = ((s32[16,1,2048]{2,1,0:T(1,128)}), s32[16,1,2048]{2,1,0:T(1,128)S(1)}, u32[]{:S(2)}, u32[]{:S(2)}) async-start(s32[16,1,2048]{2,1,0:T(1,128)} %bitcast.24), calls=%async_computation | async-start | bytes 262144 | tf_op jit(solution)/shard_map/all_to_all | solution.py:12
  225.8 73.7 %copy-start.2 = (f32[16,32]{1,0:T(8,128)S(1)}, f32[16,32]{1,0:T(8,128)}, u32[]{:S(2)}) copy-start(f32[16,32]{1,0:T(8,128)} %param.12) | copy-start | bytes 6148
  233.6 64.9 %all-to-all-start.1 = ((bf16[16,16,2048]{2,0,1:T(8,128)(2,1)}), bf16[16,16,2048]{2,0,1:T(8,128)(2,1)S(1)}, u32[]{:S(2)}, u32[]{:S(2)}) async-start(bf16[16,16,2048]{2,0,1:T(8,128)(2,1)} %bitcast.13), calls=%async_computation.1 | async-start | bytes 2097152 | tf_op jit(solution)/shard_map/all_to_all | solution.py:16
  237.3 175.1 %reduce-scatter.10.cloned.1.call-start = ((), (), s32[]{:S(2)}) async-start(), calls=%async_computation.6 | async-start | bytes 49152
  299.6 11.7 %copy-start.4 = (f32[16,64]{1,0:T(8,128)S(1)}, f32[16,64]{1,0:T(8,128)}, u32[]{:S(2)}) copy-start(f32[16,64]{1,0:T(8,128)} %get-tuple-element.209) | copy-start | bytes 12292 | tf_op jit(solution)/shard_map/while
  311.9 0.6 copy-start.5
  312.5 11.7 %copy-start.4 = (f32[16,64]{1,0:T(8,128)S(1)}, f32[16,64]{1,0:T(8,128)}, u32[]{:S(2)}) copy-start(f32[16,64]{1,0:T(8,128)} %get-tuple-element.209) | copy-start | bytes 12292 | tf_op jit(solution)/shard_map/while
  324.8 0.6 copy-start.5
  325.4 11.7 %copy-start.4 = (f32[16,64]{1,0:T(8,128)S(1)}, f32[16,64]{1,0:T(8,128)}, u32[]{:S(2)}) copy-start(f32[16,64]{1,0:T(8,128)} %get-tuple-element.209) | copy-start | bytes 12292 | tf_op jit(solution)/shard_map/while
  337.7 0.6 copy-start.5
  338.3 11.7 %copy-start.4 = (f32[16,64]{1,0:T(8,128)S(1)}, f32[16,64]{1,0:T(8,128)}, u32[]{:S(2)}) copy-start(f32[16,64]{1,0:T(8,128)} %get-tuple-element.209) | copy-start | bytes 12292 | tf_op jit(solution)/shard_map/while
  350.6 0.6 copy-start.5
  351.2 11.7 %copy-start.4 = (f32[16,64]{1,0:T(8,128)S(1)}, f32[16,64]{1,0:T(8,128)}, u32[]{:S(2)}) copy-start(f32[16,64]{1,0:T(8,128)} %get-tuple-element.209) | copy-start | bytes 12292 | tf_op jit(solution)/shard_map/while
  363.5 0.6 copy-start.5
  364.1 11.7 %copy-start.4 = (f32[16,64]{1,0:T(8,128)S(1)}, f32[16,64]{1,0:T(8,128)}, u32[]{:S(2)}) copy-start(f32[16,64]{1,0:T(8,128)} %get-tuple-element.209) | copy-start | bytes 12292 | tf_op jit(solution)/shard_map/while
  376.4 0.6 copy-start.5
  377.0 11.7 %copy-start.4 = (f32[16,64]{1,0:T(8,128)S(1)}, f32[16,64]{1,0:T(8,128)}, u32[]{:S(2)}) copy-start(f32[16,64]{1,0:T(8,128)} %get-tuple-element.209) | copy-start | bytes 12292 | tf_op jit(solution)/shard_map/while
  389.3 0.6 copy-start.5
  389.9 11.7 %copy-start.4 = (f32[16,64]{1,0:T(8,128)S(1)}, f32[16,64]{1,0:T(8,128)}, u32[]{:S(2)}) copy-start(f32[16,64]{1,0:T(8,128)} %get-tuple-element.209) | copy-start | bytes 12292 | tf_op jit(solution)/shard_map/while
  402.2 0.6 copy-start.5
  402.8 2.2 copy-start.1
  403.5 19.8 %reduce-scatter.12.cloned.1.call-start = ((), (), s32[]{:S(2)}) async-start(), calls=%async_computation.7 | async-start | bytes 49152
  404.9 29.8 %reduce-scatter.8.cloned.1.call-start = ((), (), s32[]{:S(2)}) async-start(), calls=%async_computation.5 | async-start | bytes 98304 | tf_op jit(solution)/shard_map/reduce_scatter | solution.py:87
Sparse Core Ops, SparseCore 0:
  403.6 8.7 reduce-scatter.9
  414.6 8.6 reduce-scatter.11
  426.1 8.6 reduce-scatter.7
where the time goes:
time: 523 us; the launch traced here: 520 us
  local copies, waits for them, and re-layouts  268 us (51%)
  blocking collectives  77.4 us (15%)
  other arithmetic  57.9 us (11%)
  matrix products  51.1 us (10%)
  waiting for transfers between devices  33.7 us (6%)
  between operations  13.9 us (3%)
  starting transfers between devices  12.1 us (2%)
  loops' own time  5.87 us (1%)
    gather x2, local copies, waits for them, and re-layouts, local(): picked = thickness[:, asked]  119 us
    psum x1, blocking collectives, local(): products, sums, count = lax.psum((products, sums, count), ('gx', 'gy'))  77.4 us
    scatter x1, local copies, waits for them, and re-layouts, local(): slot_depart = jnp.zeros((slots_all,), jnp.float32).at[target].set(departure)  61.1 us
    scatter x1, local copies, waits for them, and re-layouts, local(): placed = jnp.full((3, slots_all), -1, jnp.int32).at[:, target].set(stacked)  47.4 us
    dot_general x8, matrix products, accumulate(): jnp.dot(outer, hits, precision=lax.Precision.HIGHEST, preferred_element_t...  36.2 us
    slice x1, other arithmetic, local(): slot_group = placed[2]  30.9 us
    mul x8, other arithmetic, accumulate(): block[:, None, :] * block[None, :, :]  19.2 us
    unnamed x5, waiting for transfers between devices  17.5 us
  transfers between devices with their start and end apart: 5, of which 4 were waited for; matrix products, arithmetic and copies ran while one was open for 13% of the time, Pallas kernels for 0%

commit v1 on v0

--- a/solution.py
+++ b/solution.py
@@ -3,9 +3,15 @@
 import jax
 import jax.numpy as jnp
 from jax import lax
+from jax.experimental import pallas as pl
+from jax.experimental.pallas import tpu as pltpu
 from jax.sharding import PartitionSpec as P
 
 NGRP = 64
+LANES = 128
+CHUNK = 256
+TABLE_LIMIT = 24 * 1024 * 1024
+AXES = ("gx", "gy", "row")
 
 
 def send_request(wanted):
@@ -16,7 +22,7 @@
     return lax.all_to_all(picked, ("gx", "gy"), split_axis=1, concat_axis=1, tiled=True)
 
 
-def local(columns, level_weights, orbit_term, col_owner, col_local, orbit_bin, group_id, departure):
+def routed(columns, level_weights, orbit_term, col_owner, col_local, orbit_bin, group_id, departure):
     grid_x = lax.axis_size("gx")
     grid_y = lax.axis_size("gy")
     owners = grid_x * grid_y
@@ -95,6 +101,136 @@
     return (covariance, cross)
 
 
+def table_kernel(weights_ref, columns_ref, out_ref, *, npred, stripes):
+    rows = out_ref.shape[0]
+    weights = weights_ref[...]
+    parts = []
+    for s in range(stripes):
+        cols = columns_ref[:, s * rows:(s + 1) * rows]
+        parts.append(
+            lax.dot_general(weights, cols, (((0,), (0,)), ((), ())), preferred_element_type=jnp.float32)
+        )
+    out_ref[...] = jnp.concatenate(parts, axis=0).T.astype(jnp.bfloat16)
+
+
+def stats_kernel(index_ref, table_ref, packed_ref, depart_ref, orbit_ref, out_ref, wide_ref, even_ref, odd_ref,
+                 *, npred, stripes, sbits, bbits):
+    rows = table_ref.shape[0]
+    step = 512
+
+    def widen(i, carry):
+        at = pl.multiple_of(i * step, step)
+        wide_ref[pl.ds(at, step), :] = table_ref[pl.ds(at, step), :].astype(jnp.float32)
+        return carry
+
+    lax.fori_loop(0, rows // step, widen, 0)
+    nchunks = packed_ref.shape[0]
+
+    def pull(chunk, into):
+        first = chunk * CHUNK
+        for i in range(CHUNK):
+            into[i:i + 1, :] = wide_ref[pl.ds(index_ref[first + i], 1), :]
+
+    def fold(chunk, held):
+        packed = packed_ref[pl.ds(chunk, 1), :]
+        dep = depart_ref[pl.ds(chunk, 1), :]
+        stripe = packed & (stripes - 1)
+        obin = (packed >> sbits) & ((1 << bbits) - 1)
+        grp = packed >> (sbits + bbits)
+        turned = held[...].T
+        stripe = jnp.broadcast_to(stripe, (npred, CHUNK))
+        pred = turned[0:npred]
+        for s in range(1, stripes):
+            pred = jnp.where(stripe == s, turned[s * npred:(s + 1) * npred], pred)
+        orbit = orbit_ref[...]
+        obin = jnp.broadcast_to(obin, (npred, CHUNK))
+        terms = [
+            jnp.take_along_axis(orbit, obin[:, a:a + LANES], axis=1, mode="promise_in_bounds")
+            for a in range(0, CHUNK, LANES)
+        ]
+        pred = pred + jnp.concatenate(terms, axis=1)
+        hits = (lax.broadcasted_iota(jnp.int32, (NGRP, CHUNK), 0) == grp).astype(jnp.float32).astype(jnp.bfloat16)
+        pieces = [pred[i:i + 1, :] * pred for i in range(npred)]
+        pieces.append(pred * dep)
+        pieces.append(jnp.ones((16, CHUNK), jnp.float32))
+        full = jnp.concatenate(pieces, axis=0)
+        high = full.astype(jnp.bfloat16)
+        low = (full - high.astype(jnp.float32)).astype(jnp.bfloat16)
+        dims = (((1,), (1,)), ((), ()))
+        return lax.dot_general(high, hits, dims, preferred_element_type=jnp.float32) + lax.dot_general(
+            low, hits, dims, preferred_element_type=jnp.float32
+        )
+
+    out_ref[...] = jnp.zeros_like(out_ref)
+    pull(0, even_ref)
+
+    def pair(j, carry):
+        pull(2 * j + 1, odd_ref)
+        out_ref[...] += fold(2 * j, even_ref)
+        pull(jnp.minimum(2 * j + 2, nchunks - 1), even_ref)
+        out_ref[...] += fold(2 * j + 1, odd_ref)
+        return carry
+
+    lax.fori_loop(0, nchunks // 2, pair, 0)
+
+
+def local(columns, level_weights, orbit_term, col_owner, col_local, orbit_bin, group_id, departure):
+    owners = lax.axis_size("gx") * lax.axis_size("gy")
+    nrow = lax.axis_size("row")
+    levels, cdev = columns.shape
+    npred = level_weights.shape[1]
+    nbin = orbit_term.shape[1]
+    stripes = LANES // npred
+    half = cdev // nrow
+    rows = half // stripes
+    total = owners * nrow * rows
+    if total * LANES * 4 > TABLE_LIMIT:
+        return routed(
+            columns, level_weights, orbit_term, col_owner, col_local, orbit_bin, group_id, departure
+        )
+    footprints = col_local.shape[0]
+    nchunks = footprints // CHUNK
+    sbits = (stripes - 1).bit_length()
+    bbits = (nbin - 1).bit_length()
+
+    mine = lax.dynamic_slice_in_dim(columns, lax.axis_index("row") * half, half, 1)
+    piece = pl.pallas_call(
+        lambda *refs: table_kernel(*refs, npred=npred, stripes=stripes),
+        out_shape=jax.ShapeDtypeStruct((rows, LANES), jnp.bfloat16),
+        name="table",
+    )(level_weights, mine)
+    table = lax.all_gather(piece, AXES, axis=0, tiled=True)
+
+    index = (col_owner[:, 0] * nrow + col_local // half) * rows + col_local % rows
+    stripe = (col_local % half) // rows
+    packed = stripe | (orbit_bin << sbits) | (group_id << (sbits + bbits))
+    orbit = jnp.pad(orbit_term, ((0, 0), (0, LANES - nbin)))
+    vmem = pl.BlockSpec(memory_space=pltpu.VMEM)
+    height = npred * npred + npred + 16
+    stats = pl.pallas_call(
+        lambda *refs: stats_kernel(*refs, npred=npred, stripes=stripes, sbits=sbits, bbits=bbits),
+        out_shape=jax.ShapeDtypeStruct((height, NGRP), jnp.float32),
+        in_specs=[pl.BlockSpec(memory_space=pltpu.SMEM), vmem, vmem, vmem, vmem],
+        out_specs=vmem,
+        scratch_shapes=[
+            pltpu.VMEM((total, LANES), jnp.float32),
+            pltpu.VMEM((CHUNK, LANES), jnp.float32),
+            pltpu.VMEM((CHUNK, LANES), jnp.float32),
+        ],
+        compiler_params=pltpu.CompilerParams(vmem_limit_bytes=40 * 1024 * 1024),
+        name="stats",
+    )(index, table, packed.reshape(nchunks, CHUNK), departure.reshape(nchunks, CHUNK), orbit)
+
+    share = NGRP // nrow
+    stats = lax.psum_scatter(stats, "row", scatter_dimension=1, tiled=True)
+    stats = lax.psum(stats, ("gx", "gy"))
+    square = npred * npred
+    scale = 1.0 / (stats[square + npred:square + npred + 1] + 1.0)
+    covariance = (stats[:square] * scale).reshape(npred, npred, share)
+    cross = stats[square:square + npred] * scale
+    return (covariance, cross)
+
+
 def solution(mesh):
     in_specs = (
         P(None, ("gx", "gy")),

time: 523 us -> 203 us (0.39)
  local copies, waits for them, and re-layouts: 268 us -> 6.58 us
  other arithmetic: 57.9 us -> 1.46 us
  matrix products: 51.1 us -> 0 us
  waiting for transfers between devices: 33.7 us -> 70.7 us
  Pallas kernels: 0 us -> 29.8 us
  starting transfers between devices: 12.1 us -> 0.08 us
  loops' own time: 5.87 us -> 0 us
    gather x2 -> x0, local copies, waits for them, and re-layouts: 119 us -> none  [local(): picked = thickness[:, asked]]
    scatter x2 -> x0, local copies, waits for them, and re-layouts: 109 us -> none  [the longest x1 61.1 us: local(): slot_depart = jnp.zeros((slots_all,), jnp.float32).at[target].set(departure)]
    all_gather x0 -> x1, waiting for transfers between devices: none -> 64.2 us  [local(): table = lax.all_gather(piece, AXES, axis=0, tiled=True)]
    dot_general x25 -> x0, matrix products: 51.1 us -> none  [the longest x8 36.2 us: accumulate(): jnp.dot(outer, hits, precision=lax.Precision.HIGHEST, preferred_element_t...]
    slice x1 -> x0, other arithmetic: 30.9 us -> none  [local(): slot_group = placed[2]]
    pallas_call x0 -> x2, Pallas kernels: none -> 29.8 us  [the longest x1 27.5 us: local(): pl.pallas_call(lambda *refs: stats_kernel(*refs, npred=npred, stripes=str...]
    dynamic_slice x32 -> x1, local copies, waits for them, and re-layouts: 22.7 us -> 1.1 us  [local(): lax.dynamic_slice_in_dim(columns, lax.axis_index('row') * half, half, 1)]
    mul x11 -> x4, other arithmetic: 19.9 us -> 1.33 us  [the longest x2 0.67 us: local(): covariance = (stats[:square] * scale).reshape(npred, npred, share)]
  transfers between devices with their start and end apart: 5 -> 2, of which waited for: 4 -> 2; matrix products, arithmetic and copies ran while one was open for 13% -> 0% of each run, Pallas kernels for 0% -> 0%
where the time goes in v1:
time: 203 us
  blocking collectives  80.1 us (39%)
  waiting for transfers between devices  70.7 us (35%)
  Pallas kernels  29.8 us (15%)
  between operations  14.2 us (7%)
  local copies, waits for them, and re-layouts  6.58 us (3%)
    psum x1, blocking collectives, local(): stats = lax.psum(stats, ('gx', 'gy'))  80.1 us
    all_gather x1, waiting for transfers between devices, local(): table = lax.all_gather(piece, AXES, axis=0, tiled=True)  64.2 us
    pallas_call x1, Pallas kernels, local(): pl.pallas_call(lambda *refs: stats_kernel(*refs, npred=npred, stripes=str...  27.5 us
    unnamed x3, waiting for transfers between devices  6.52 us
    unnamed x19, local copies, waits for them, and re-layouts  5.43 us
  transfers between devices with their start and end apart: 2, of which 2 were waited for; matrix products, arithmetic and copies ran while one was open for 0% of the time, Pallas kernels for 0%

profile of v1, /device:TPU:0, one launch (start us, length us, event | category | flops | bytes accessed | tf_op | source)
XLA Modules:
  0.0 202.9 jit_solution(5623650005801251500)
XLA Ops:
  7.2 0.0 copy-start
  7.2 0.0 copy-start.2
  7.2 0.0 copy-start.3
  7.2 0.0 copy-start.4
  7.2 0.0 copy-start.5
  7.2 0.0 copy-start.6
  7.2 0.0 copy-start.7
  7.2 0.0 all-gather.2.cloned.1.call-start
  7.3 1.6 copy.11.refs_0_
  8.8 0.0 copy-done
  8.9 1.1 constant_dynamic-slice_fusion.refs_1_
  10.0 2.3 %table.1 = bf16[512,128]{1,0:T(8,128)(2,1)} custom-call(bf16[137,16]{1,0:T(8,128)(2,1)} %copy.11.refs_0_, bf16[137,4096]{1,0:T(8,128)(2,1)} %constant_dynamic-slice_fusion.refs_1_), custom_call_target="tpu_custom_call" | custom-call | tf_op jit(solution)/shard_map/table/pallas_call | solution.py:197
  12.3 0.0 all-gather.2.cloned.1.call-update
  12.3 0.0 reduce-scatter.4.cloned.1.call-start
  12.4 0.0 copy-done.2
  12.4 0.0 copy-done.3
  12.4 0.1 broadcast_multiply_fusion
  12.5 0.0 copy-done.4
  12.5 0.0 copy-done.5
  12.5 0.0 copy-done.6
  12.5 0.1 fusion.5
  12.7 0.0 copy-done.7
  12.7 64.2 %all-gather.2.cloned.1.call-done.refs_1_ = bf16[16384,128]{1,0:T(8,128)(2,1)} async-done(((bf16[512,128]{1,0:T(8,128)(2,1)}), bf16[16384,128]{1,0:T(8,128)(2,1)}) %all-gather.2.cloned.1.call-update) | async-done | bytes 4194320 | tf_op jit(solution)/shard_map/all_gather | solution.py:202
  76.9 2.2 %copy-done.1 = bf16[16384,128]{1,0:T(8,128)(2,1)S(1)} copy-done((bf16[16384,128]{1,0:T(8,128)(2,1)S(1)}, bf16[16384,128]{1,0:T(8,128)(2,1)}, u32[]{:S(2)}) %copy-start.1) | copy-done | bytes 4194328
  79.0 27.5 %stats.1 = f32[288,64]{1,0:T(8,128)S(1)} custom-call(s32[16384]{0:T(1024)S(1)} %get-tuple-element.3.refs_0_, bf16[16384,128]{1,0:T(8,128)(2,1)S(1)} %copy-done.1, s32[64,256]{1,0:T(8,128)S(1)} %reshape.15.refs_2_, f32[64,256]{1,0:T(8,128)S(1)} %reshape.16.refs_3_, f32[16,128]{1,0:T(8,128)S(1)} %pad.4.refs_4_), custom_call_target="tpu_custom_call" | custom-call | tf_op jit(solution)/shard_map/stats/pallas_call | solution.py:210
  106.6 0.8 copy.12
  107.3 0.0 reduce-scatter.4.cloned.1.call-update
  107.3 6.5 %reduce-scatter.4.cloned.1.call-done = f32[32,288]{1,0:T(8,128)} async-done(((f32[64,288]{1,0:T(8,128)}), f32[32,288]{1,0:T(8,128)}) %reduce-scatter.4.cloned.1.call-update) | async-done | bytes 36880
  113.8 0.9 copy.13
  114.7 80.1 %psum.7 = f32[288,32]{1,0:T(8,128)S(1)} all-reduce(f32[288,32]{1,0:T(8,128)S(1)} %copy.13), channel_id=1, replica_groups=mesh['gx'=4,'gy'=4,'row'=2] {'gx','gy'}, use_global_device_ids=true, to_apply=%region_1.2 | all-reduce | flops 9216 | bytes 73728 | tf_op jit(solution)/shard_map/psum | solution.py:226
  194.8 0.6 slice_multiply_fusion.1
  195.4 0.7 slice_multiply_fusion
  (5 shorter events, 0.1 us)
Async XLA Ops:
  7.2 1.7 copy-start
  7.2 5.2 %copy-start.2 = (f32[16384]{0:T(1024)S(1)}, f32[16384]{0:T(1024)}, u32[]{:S(2)}) copy-start(f32[16384]{0:T(1024)} %param.15) | copy-start | bytes 196612
  7.2 5.2 %copy-start.3 = (s32[16384,1]{0,1:T(1,128)S(1)}, s32[16384,1]{0,1:T(1,128)}, u32[]{:S(2)}) copy-start(s32[16384,1]{0,1:T(1,128)} %param.11) | copy-start | bytes 196612
  7.2 5.3 %copy-start.4 = (s32[16384]{0:T(1024)S(1)}, s32[16384]{0:T(1024)}, u32[]{:S(2)}) copy-start(s32[16384]{0:T(1024)} %param.14) | copy-start | bytes 196612
  7.2 5.3 %copy-start.5 = (s32[16384]{0:T(1024)S(1)}, s32[16384]{0:T(1024)}, u32[]{:S(2)}) copy-start(s32[16384]{0:T(1024)} %param.13) | copy-start | bytes 196612
  7.2 5.3 %copy-start.6 = (s32[16384]{0:T(1024)S(1)}, s32[16384]{0:T(1024)}, u32[]{:S(2)}) copy-start(s32[16384]{0:T(1024)} %param.12) | copy-start | bytes 196612
  7.2 5.4 %copy-start.7 = (f32[16,32]{1,0:T(8,128)S(1)}, f32[16,32]{1,0:T(8,128)}, u32[]{:S(2)}) copy-start(f32[16,32]{1,0:T(8,128)} %param.10) | copy-start | bytes 6148
  7.2 69.6 %all-gather.2.cloned.1.call-start = ((), (), s32[]{:S(2)}) async-start(), calls=%async_computation.1 | async-start | bytes 4325376 | tf_op jit(solution)/shard_map/all_gather | solution.py:202
  12.3 101.5 %reduce-scatter.4.cloned.1.call-start = ((), (), s32[]{:S(2)}) async-start(), calls=%async_computation.2 | async-start | bytes 147456
  76.9 2.2 %copy-start.1 = (bf16[16384,128]{1,0:T(8,128)(2,1)S(1)}, bf16[16384,128]{1,0:T(8,128)(2,1)}, u32[]{:S(2)}) copy-start(bf16[16384,128]{1,0:T(8,128)(2,1)} %all-gather.2.cloned.1.call-done.refs_1_) | copy-start | bytes 12582916
Sparse Core Ops, SparseCore 0:
  12.4 64.3 all-gather.1
  107.5 6.3 reduce-scatter.3

commit v2 on v1

--- a/solution.py
+++ b/solution.py
@@ -101,8 +101,27 @@
     return (covariance, cross)
 
 
-def table_kernel(weights_ref, columns_ref, out_ref, *, npred, stripes):
-    rows = out_ref.shape[0]
+def grid_place(gx, gy, row, n_gy, n_row):
+    return (gx * n_gy + gy) * n_row + row
+
+
+def table_kernel(weights_ref, columns_ref, out_ref, send_sems, recv_sems, *, npred, stripes, n_gy, n_row):
+    rows = columns_ref.shape[1] // stripes
+    gx, gy, row = lax.axis_index("gx"), lax.axis_index("gy"), lax.axis_index("row")
+    low_bit, high_bit = gx % 2, gx // 2
+    low_step, high_step = 1 - 2 * low_bit, 2 * (1 - 2 * high_bit)
+    gx_a = gx + (1 - row) * low_step + row * high_step
+    gx_b = gx + row * low_step + (1 - row) * high_step
+    gx_ab = gx + low_step + high_step
+    gys = [(gy + i) % n_gy for i in range(n_gy)]
+    along = [(gx, gys[i], row) for i in range(1, n_gy)]
+    to_a, to_b, mate = (gx_a, gy, row), (gx_b, gy, row), (gx, gy, 1 - row)
+    peers = along + [to_a, to_b, mate]
+
+    barrier = pltpu.get_barrier_semaphore()
+    for peer in peers:
+        pl.semaphore_signal(barrier, inc=1, device_id=peer, device_id_type=pl.DeviceIdType.MESH)
+
     weights = weights_ref[...]
     parts = []
     for s in range(stripes):
@@ -110,11 +129,133 @@
         parts.append(
             lax.dot_general(weights, cols, (((0,), (0,)), ((), ())), preferred_element_type=jnp.float32)
         )
-    out_ref[...] = jnp.concatenate(parts, axis=0).T.astype(jnp.bfloat16)
+    own = grid_place(gx, gy, row, n_gy, n_row)
+    out_ref[pl.ds(pl.multiple_of(own * rows, rows), rows), :] = (
+        jnp.concatenate(parts, axis=0).T.astype(jnp.bfloat16)
+    )
+    pl.semaphore_wait(barrier, len(peers))
+
+    sent = []
+
+    def copy(block, peer, number):
+        at = out_ref.at[pl.ds(pl.multiple_of(block * rows, rows), rows), :]
+        return pltpu.make_async_remote_copy(
+            src_ref=at, dst_ref=at, send_sem=send_sems.at[number], recv_sem=recv_sems.at[block],
+            device_id=peer, device_id_type=pl.DeviceIdType.MESH,
+        )
+
+    def send(block, targets):
+        for peer in targets:
+            c = copy(block, peer, len(sent))
+            c.start()
+            sent.append(c)
+
+    def arrive(block):
+        copy(block, mate, 0).wait_recv()
+
+    def place(x, y):
+        return grid_place(x, y, row, n_gy, n_row)
+
+    order = [0] + sorted(range(1, n_gy), key=lambda i: min(i, n_gy - i))
+    send(own, along + [to_a, to_b, mate])
+    arrive(place(gx_a, gy))
+    send(place(gx_a, gy), [to_b, mate])
+    arrive(place(gx_b, gy))
+    send(place(gx_b, gy), [mate])
+    for i in order[1:]:
+        arrive(place(gx, gys[i]))
+        send(place(gx, gys[i]), [to_a, to_b, mate])
+    for i in order[1:]:
+        arrive(place(gx_a, gys[i]))
+        send(place(gx_a, gys[i]), [to_b, mate])
+    arrive(place(gx_ab, gy))
+    send(place(gx_ab, gy), [mate])
+    for i in order[1:]:
+        arrive(place(gx_b, gys[i]))
+        send(place(gx_b, gys[i]), [mate])
+        arrive(place(gx_ab, gys[i]))
+        send(place(gx_ab, gys[i]), [mate])
+    for x in (gx, gx_a, gx_b, gx_ab):
+        for y in gys:
+            arrive(grid_place(x, y, 1 - row, n_gy, n_row))
+    for c in sent:
+        c.wait_send()
+
+
+def reduce_kernel(stats_ref, cov_ref, cross_ref, parts_ref, whole_ref, send_a, recv_a, send_b, recv_b,
+                  *, npred, n_gx, n_gy, n_row, height):
+    gx, gy, row = lax.axis_index("gx"), lax.axis_index("gy"), lax.axis_index("row")
+    owners = n_gx * n_gy
+    piece = whole_ref.shape[0] // owners
+    mine = gx * n_gy + gy
+    others = []
+    for dx in range(n_gx):
+        for dy in range(n_gy):
+            for dr in range(n_row):
+                if dx or dy or dr:
+                    others.append(((gx + dx) % n_gx, (gy + dy) % n_gy, (row + dr) % n_row))
+    barrier = pltpu.get_barrier_semaphore()
+    for peer in others:
+        pl.semaphore_signal(barrier, inc=1, device_id=peer, device_id_type=pl.DeviceIdType.MESH)
+    pl.semaphore_wait(barrier, len(others))
+
+    def rows_of(owner):
+        return pl.ds(pl.multiple_of(owner * piece, piece), piece)
+
+    me = mine * n_row + row
+    first = []
+    for k, peer in enumerate(others):
+        owner = peer[0] * n_gy + peer[1]
+        c = pltpu.make_async_remote_copy(
+            src_ref=stats_ref.at[peer[2], rows_of(owner), :], dst_ref=parts_ref.at[me],
+            send_sem=send_a.at[k], recv_sem=recv_a.at[me],
+            device_id=peer, device_id_type=pl.DeviceIdType.MESH,
+        )
+        c.start()
+        first.append(c)
+    total = stats_ref[row, rows_of(mine), :]
+    for k, peer in enumerate(others):
+        who = grid_place(peer[0], peer[1], peer[2], n_gy, n_row)
+        pltpu.make_async_remote_copy(
+            src_ref=stats_ref.at[row, rows_of(mine), :], dst_ref=parts_ref.at[who],
+            send_sem=send_a.at[k], recv_sem=recv_a.at[who],
+            device_id=peer, device_id_type=pl.DeviceIdType.MESH,
+        ).wait_recv()
+        total = total + parts_ref[who]
+    whole_ref[rows_of(mine), :] = total
+    second = []
+    for k, peer in enumerate(others):
+        if k % n_row == n_row - 1:
+            c = pltpu.make_async_remote_copy(
+                src_ref=whole_ref.at[rows_of(mine), :], dst_ref=whole_ref.at[rows_of(mine), :],
+                send_sem=send_b.at[len(second)], recv_sem=recv_b.at[mine],
+                device_id=peer, device_id_type=pl.DeviceIdType.MESH,
+            )
+            c.start()
+            second.append((c, peer))
+    for k, (c, peer) in enumerate(second):
+        owner = peer[0] * n_gy + peer[1]
+        pltpu.make_async_remote_copy(
+            src_ref=whole_ref.at[rows_of(owner), :], dst_ref=whole_ref.at[rows_of(owner), :],
+            send_sem=send_b.at[k], recv_sem=recv_b.at[owner],
+            device_id=peer, device_id_type=pl.DeviceIdType.MESH,
+        ).wait_recv()
+    share = cov_ref.shape[1]
+    folds = LANES // share
+    part = height // folds
+    flat = jnp.concatenate([whole_ref[0:part, q * share:(q + 1) * share] for q in range(folds)], axis=0)
+    square = npred * npred
+    scale = 1.0 / (flat[square + npred:square + npred + 1] + 1.0)
+    cov_ref[...] = flat[:square] * scale
+    cross_ref[...] = flat[square:square + npred] * scale
+    for c in first:
+        c.wait_send()
+    for c, _ in second:
+        c.wait_send()
 
 
 def stats_kernel(index_ref, table_ref, packed_ref, depart_ref, orbit_ref, out_ref, wide_ref, even_ref, odd_ref,
-                 *, npred, stripes, sbits, bbits):
+                 acc_ref, *, npred, stripes, sbits, bbits):
     rows = table_ref.shape[0]
     step = 512
 
@@ -161,21 +302,31 @@
             low, hits, dims, preferred_element_type=jnp.float32
         )
 
-    out_ref[...] = jnp.zeros_like(out_ref)
+    acc_ref[...] = jnp.zeros_like(acc_ref)
     pull(0, even_ref)
 
     def pair(j, carry):
         pull(2 * j + 1, odd_ref)
-        out_ref[...] += fold(2 * j, even_ref)
+        acc_ref[...] += fold(2 * j, even_ref)
         pull(jnp.minimum(2 * j + 2, nchunks - 1), even_ref)
-        out_ref[...] += fold(2 * j + 1, odd_ref)
+        acc_ref[...] += fold(2 * j + 1, odd_ref)
         return carry
 
     lax.fori_loop(0, nchunks // 2, pair, 0)
+    halves = out_ref.shape[0]
+    share = NGRP // halves
+    folds = LANES // share
+    part = acc_ref.shape[0] // folds
+    out_ref[...] = jnp.zeros_like(out_ref)
+    for h in range(halves):
+        out_ref[h, 0:part, :] = jnp.concatenate(
+            [acc_ref[q * part:(q + 1) * part, h * share:(h + 1) * share] for q in range(folds)], axis=1
+        )
 
 
 def local(columns, level_weights, orbit_term, col_owner, col_local, orbit_bin, group_id, departure):
-    owners = lax.axis_size("gx") * lax.axis_size("gy")
+    n_gx, n_gy = lax.axis_size("gx"), lax.axis_size("gy")
+    owners = n_gx * n_gy
     nrow = lax.axis_size("row")
     levels, cdev = columns.shape
     npred = level_weights.shape[1]
@@ -184,7 +335,7 @@
     half = cdev // nrow
     rows = half // stripes
     total = owners * nrow * rows
-    if total * LANES * 4 > TABLE_LIMIT:
+    if total * LANES * 4 > TABLE_LIMIT or n_gx != 4 or nrow != 2:
         return routed(
             columns, level_weights, orbit_term, col_owner, col_local, orbit_bin, group_id, departure
         )
@@ -194,41 +345,67 @@
     bbits = (nbin - 1).bit_length()
 
     mine = lax.dynamic_slice_in_dim(columns, lax.axis_index("row") * half, half, 1)
-    piece = pl.pallas_call(
-        lambda *refs: table_kernel(*refs, npred=npred, stripes=stripes),
-        out_shape=jax.ShapeDtypeStruct((rows, LANES), jnp.bfloat16),
+    vmem = pl.BlockSpec(memory_space=pltpu.VMEM)
+    sends = n_gy - 1 + 3 + (n_gy - 1) * 3 + n_gy * 2 + n_gy * 2
+    table = pl.pallas_call(
+        lambda *refs: table_kernel(*refs, npred=npred, stripes=stripes, n_gy=n_gy, n_row=nrow),
+        out_shape=jax.ShapeDtypeStruct((total, LANES), jnp.bfloat16),
+        in_specs=[vmem, vmem],
+        out_specs=vmem,
+        scratch_shapes=[
+            pltpu.SemaphoreType.DMA((sends,)),
+            pltpu.SemaphoreType.DMA((owners * nrow,)),
+        ],
+        compiler_params=pltpu.CompilerParams(collective_id=0, has_side_effects=True),
         name="table",
     )(level_weights, mine)
-    table = lax.all_gather(piece, AXES, axis=0, tiled=True)
 
     index = (col_owner[:, 0] * nrow + col_local // half) * rows + col_local % rows
     stripe = (col_local % half) // rows
     packed = stripe | (orbit_bin << sbits) | (group_id << (sbits + bbits))
     orbit = jnp.pad(orbit_term, ((0, 0), (0, LANES - nbin)))
-    vmem = pl.BlockSpec(memory_space=pltpu.VMEM)
     height = npred * npred + npred + 16
+    folds = LANES * nrow // NGRP
+    tall = -(-height // (folds * owners * 8)) * owners * 8
     stats = pl.pallas_call(
         lambda *refs: stats_kernel(*refs, npred=npred, stripes=stripes, sbits=sbits, bbits=bbits),
-        out_shape=jax.ShapeDtypeStruct((height, NGRP), jnp.float32),
+        out_shape=jax.ShapeDtypeStruct((nrow, tall, LANES), jnp.float32),
         in_specs=[pl.BlockSpec(memory_space=pltpu.SMEM), vmem, vmem, vmem, vmem],
         out_specs=vmem,
         scratch_shapes=[
             pltpu.VMEM((total, LANES), jnp.float32),
             pltpu.VMEM((CHUNK, LANES), jnp.float32),
             pltpu.VMEM((CHUNK, LANES), jnp.float32),
+            pltpu.VMEM((height, NGRP), jnp.float32),
         ],
         compiler_params=pltpu.CompilerParams(vmem_limit_bytes=40 * 1024 * 1024),
         name="stats",
     )(index, table, packed.reshape(nchunks, CHUNK), departure.reshape(nchunks, CHUNK), orbit)
 
     share = NGRP // nrow
-    stats = lax.psum_scatter(stats, "row", scatter_dimension=1, tiled=True)
-    stats = lax.psum(stats, ("gx", "gy"))
-    square = npred * npred
-    scale = 1.0 / (stats[square + npred:square + npred + 1] + 1.0)
-    covariance = (stats[:square] * scale).reshape(npred, npred, share)
-    cross = stats[square:square + npred] * scale
-    return (covariance, cross)
+    devices = owners * nrow
+    covariance, cross = pl.pallas_call(
+        lambda *refs: reduce_kernel(
+            *refs, npred=npred, n_gx=n_gx, n_gy=n_gy, n_row=nrow, height=height
+        ),
+        out_shape=(
+            jax.ShapeDtypeStruct((npred * npred, share), jnp.float32),
+            jax.ShapeDtypeStruct((npred, share), jnp.float32),
+        ),
+        in_specs=[vmem],
+        out_specs=(vmem, vmem),
+        scratch_shapes=[
+            pltpu.VMEM((devices, tall // owners, LANES), jnp.float32),
+            pltpu.VMEM((tall, LANES), jnp.float32),
+            pltpu.SemaphoreType.DMA((devices - 1,)),
+            pltpu.SemaphoreType.DMA((devices,)),
+            pltpu.SemaphoreType.DMA((owners - 1,)),
+            pltpu.SemaphoreType.DMA((owners,)),
+        ],
+        compiler_params=pltpu.CompilerParams(collective_id=1, has_side_effects=True),
+        name="reduce",
+    )(stats)
+    return (covariance.reshape(npred, npred, share), cross)
 
 
 def solution(mesh):

time: 203 us -> 90.1 us (0.44)
  blocking collectives: 80.1 us -> 0 us
  waiting for transfers between devices: 70.7 us -> 0 us
  Pallas kernels: 29.8 us -> 79.6 us
  between operations: 14.2 us -> 0.8 us
  local copies, waits for them, and re-layouts: 6.58 us -> 9.23 us
    psum x1 -> x0, blocking collectives: 80.1 us -> none  [local(): stats = lax.psum(stats, ('gx', 'gy'))]
    all_gather x1 -> x0, waiting for transfers between devices: 64.2 us -> none  [local(): table = lax.all_gather(piece, AXES, axis=0, tiled=True)]
    pallas_call x1, Pallas kernels: 2.32 us -> 33.6 us  [local(): pl.pallas_call(lambda *refs: table_kernel(*refs, npred=npred, stripes=str...]
    pallas_call x0 -> x1, Pallas kernels: none -> 18.4 us  [local(): pl.pallas_call(lambda *refs: reduce_kernel(*refs, npred=npred, n_gx=n_gx,...]
    unnamed x3 -> x0, waiting for transfers between devices: 6.52 us -> none
    unnamed x19 -> x23, local copies, waits for them, and re-layouts: 5.43 us -> 8.09 us
  transfers between devices with their start and end apart: 2 -> 0, of which waited for: 2 -> 0; matrix products, arithmetic and copies ran while one was open for 0% -> 0% of each run, Pallas kernels for 0% -> 0%
where the time goes in v2:
time: 90.1 us; the launch traced here: 89.8 us
  Pallas kernels  79.6 us (88%)
  local copies, waits for them, and re-layouts  9.23 us (10%)
    pallas_call x1, Pallas kernels, local(): pl.pallas_call(lambda *refs: table_kernel(*refs, npred=npred, stripes=str...  33.6 us
    pallas_call x1, Pallas kernels, local(): pl.pallas_call(lambda *refs: stats_kernel(*refs, npred=npred, stripes=str...  27.6 us
    pallas_call x1, Pallas kernels, local(): pl.pallas_call(lambda *refs: reduce_kernel(*refs, npred=npred, n_gx=n_gx,...  18.4 us
    unnamed x23, local copies, waits for them, and re-layouts  8.09 us

profile of v2, /device:TPU:0, one launch (start us, length us, event | category | flops | bytes accessed | tf_op | source)
XLA Modules:
  0.0 89.8 jit_solution(16804404300323197003)
XLA Ops:
  0.6 0.0 copy-start
  0.6 0.0 copy-start.9
  0.7 1.6 %copy-done = bf16[137,8192]{1,0:T(8,128)(2,1)S(1)} copy-done((bf16[137,8192]{1,0:T(8,128)(2,1)S(1)}, bf16[137,8192]{1,0:T(8,128)(2,1)}, u32[]{:S(2)}) %copy-start) | copy-done | bytes 2244632
  2.3 1.1 %constant_dynamic-slice_fusion.refs_1_ = bf16[137,4096]{1,0:T(8,128)(2,1)} fusion(bf16[137,8192]{1,0:T(8,128)(2,1)S(1)} %copy-done, s32[]{:T(128)S(6)} %select_n.24), kind=kLoop, calls=%fused_computation.24 | loop fusion | bytes 2244612 | tf_op jit(solution)/shard_map/dynamic_slice | solution.py:347
  3.4 0.0 copy-done.9
  3.4 0.7 copy.10.refs_0_
  4.1 0.0 copy-start.3
  4.1 0.0 copy-start.5
  4.1 0.0 copy-start.6
  4.1 0.0 copy-start.7
  4.1 0.0 copy-start.4
  4.1 0.0 copy-start.8
  4.1 33.6 %table.1.refs_1_ = bf16[16384,128]{1,0:T(8,128)(2,1)} custom-call(bf16[137,16]{1,0:T(8,128)(2,1)} %copy.10.refs_0_, bf16[137,4096]{1,0:T(8,128)(2,1)} %constant_dynamic-slice_fusion.refs_1_), custom_call_target="tpu_custom_call" | custom-call | tf_op jit(solution)/shard_map/table/pallas_call | solution.py:350
  37.7 0.0 copy-done.3
  37.7 0.1 broadcast_multiply_fusion
  37.8 0.0 copy-done.5
  37.8 0.0 copy-done.6
  37.8 0.0 copy-done.7
  37.8 0.1 fusion.5
  38.0 0.0 copy-done.4
  38.0 0.0 copy-done.8
  38.1 0.0 copy-start.1
  38.1 2.2 %copy-done.1 = bf16[16384,128]{1,0:T(8,128)(2,1)S(1)} copy-done((bf16[16384,128]{1,0:T(8,128)(2,1)S(1)}, bf16[16384,128]{1,0:T(8,128)(2,1)}, u32[]{:S(2)}) %copy-start.1) | copy-done | bytes 4194328
  40.2 27.6 %stats.1.refs_0_ = f32[2,128,128]{2,1,0:T(8,128)S(1)} custom-call(s32[16384]{0:T(1024)S(1)} %get-tuple-element.7.refs_0_, bf16[16384,128]{1,0:T(8,128)(2,1)S(1)} %copy-done.1, s32[64,256]{1,0:T(8,128)S(1)} %reshape.15.refs_2_, f32[64,256]{1,0:T(8,128)S(1)} %reshape.16.refs_3_, f32[16,128]{1,0:T(8,128)S(1)} %pad.4.refs_4_), custom_call_target="tpu_custom_call" | custom-call | tf_op jit(solution)/shard_map/stats/pallas_call | solution.py:370
  67.9 0.0 copy-start.2
  67.9 0.6 copy-done.2
  68.5 18.4 %reduce.1 = (f32[256,32]{1,0:T(8,128)}, f32[16,32]{1,0:T(8,128)}) custom-call(f32[2,128,128]{2,1,0:T(8,128)} %copy-done.2), custom_call_target="tpu_custom_call" | custom-call | tf_op jit(solution)/shard_map/reduce/pallas_call | solution.py:387
  87.0 1.6 %copy.13 = f32[16,16,32]{2,1,0:T(8,128)} copy(f32[16,16,32]{2,1,0:T(8,128)} %bitcast.3) | data formatting | bytes 65536
  88.5 1.3 %copy.14 = f32[16,32]{1,0:T(8,128)} copy(f32[16,32]{1,0:T(8,128)} %get-tuple-element.11) | data formatting | bytes 4096
  (3 shorter events, 0.0 us)
Async XLA Ops:
  0.6 1.7 %copy-start = (bf16[137,8192]{1,0:T(8,128)(2,1)S(1)}, bf16[137,8192]{1,0:T(8,128)(2,1)}, u32[]{:S(2)}) copy-start(bf16[137,8192]{1,0:T(8,128)(2,1)} %param.8) | copy-start | bytes 6733828
  0.6 2.7 %copy-start.9 = (bf16[137,16]{0,1:T(8,128)(2,1)S(1)}, bf16[137,16]{0,1:T(8,128)(2,1)}, u32[]{:S(2)}) copy-start(bf16[137,16]{0,1:T(8,128)(2,1)} %param.9) | copy-start | bytes 13156
  4.1 33.6 %copy-start.3 = (s32[16384,1]{0,1:T(1,128)S(1)}, s32[16384,1]{0,1:T(1,128)}, u32[]{:S(2)}) copy-start(s32[16384,1]{0,1:T(1,128)} %param.11) | copy-start | bytes 196612
  4.1 33.7 %copy-start.5 = (s32[16384]{0:T(1024)S(1)}, s32[16384]{0:T(1024)}, u32[]{:S(2)}) copy-start(s32[16384]{0:T(1024)} %param.14) | copy-start | bytes 196612
  4.1 33.7 %copy-start.6 = (s32[16384]{0:T(1024)S(1)}, s32[16384]{0:T(1024)}, u32[]{:S(2)}) copy-start(s32[16384]{0:T(1024)} %param.13) | copy-start | bytes 196612
  4.1 33.7 %copy-start.7 = (s32[16384]{0:T(1024)S(1)}, s32[16384]{0:T(1024)}, u32[]{:S(2)}) copy-start(s32[16384]{0:T(1024)} %param.12) | copy-start | bytes 196612
  4.1 33.9 %copy-start.4 = (f32[16384]{0:T(1024)S(1)}, f32[16384]{0:T(1024)}, u32[]{:S(2)}) copy-start(f32[16384]{0:T(1024)} %param.15) | copy-start | bytes 196612
  4.1 33.9 %copy-start.8 = (f32[16,32]{1,0:T(8,128)S(1)}, f32[16,32]{1,0:T(8,128)}, u32[]{:S(2)}) copy-start(f32[16,32]{1,0:T(8,128)} %param.10) | copy-start | bytes 6148
  38.1 2.2 %copy-start.1 = (bf16[16384,128]{1,0:T(8,128)(2,1)S(1)}, bf16[16384,128]{1,0:T(8,128)(2,1)}, u32[]{:S(2)}) copy-start(bf16[16384,128]{1,0:T(8,128)(2,1)} %table.1.refs_1_) | copy-start | bytes 12582916
  67.9 0.7 copy-start.2

commit v3 on v2

--- a/solution.py
+++ b/solution.py
@@ -105,7 +105,7 @@
     return (gx * n_gy + gy) * n_row + row
 
 
-def table_kernel(weights_ref, columns_ref, out_ref, send_sems, recv_sems, *, npred, stripes, n_gy, n_row):
+def table_kernel(weights_ref, all_columns_ref, out_ref, columns_ref, load_sem, send_sems, recv_sems, *, npred, stripes, n_gy, n_row):
     rows = columns_ref.shape[1] // stripes
     gx, gy, row = lax.axis_index("gx"), lax.axis_index("gy"), lax.axis_index("row")
     low_bit, high_bit = gx % 2, gx // 2
@@ -114,20 +114,27 @@
     gx_b = gx + row * low_step + (1 - row) * high_step
     gx_ab = gx + low_step + high_step
     gys = [(gy + i) % n_gy for i in range(n_gy)]
-    along = [(gx, gys[i], row) for i in range(1, n_gy)]
+    order = sorted(range(1, n_gy), key=lambda i: min(i, n_gy - i))
+    along = [(gx, gys[i], row) for i in order]
     to_a, to_b, mate = (gx_a, gy, row), (gx_b, gy, row), (gx, gy, 1 - row)
     peers = along + [to_a, to_b, mate]
 
+    half = columns_ref.shape[1]
+    load = pltpu.make_async_copy(
+        all_columns_ref.at[:, pl.ds(pl.multiple_of(row * half, half), half)], columns_ref, load_sem
+    )
+    load.start()
     barrier = pltpu.get_barrier_semaphore()
     for peer in peers:
         pl.semaphore_signal(barrier, inc=1, device_id=peer, device_id_type=pl.DeviceIdType.MESH)
+    load.wait()
 
     weights = weights_ref[...]
     parts = []
     for s in range(stripes):
         cols = columns_ref[:, s * rows:(s + 1) * rows]
         parts.append(
-            lax.dot_general(weights, cols, (((0,), (0,)), ((), ())), preferred_element_type=jnp.float32)
+            lax.dot_general(weights, cols, (((1,), (0,)), ((), ())), preferred_element_type=jnp.float32)
         )
     own = grid_place(gx, gy, row, n_gy, n_row)
     out_ref[pl.ds(pl.multiple_of(own * rows, rows), rows), :] = (
@@ -156,25 +163,33 @@
     def place(x, y):
         return grid_place(x, y, row, n_gy, n_row)
 
-    order = [0] + sorted(range(1, n_gy), key=lambda i: min(i, n_gy - i))
-    send(own, along + [to_a, to_b, mate])
-    arrive(place(gx_a, gy))
-    send(place(gx_a, gy), [to_b, mate])
-    arrive(place(gx_b, gy))
-    send(place(gx_b, gy), [mate])
-    for i in order[1:]:
+    def from_along(i):
         arrive(place(gx, gys[i]))
-        send(place(gx, gys[i]), [to_a, to_b, mate])
-    for i in order[1:]:
+        send(place(gx, gys[i]), [to_b, to_a, mate])
+
+    def from_a(i):
         arrive(place(gx_a, gys[i]))
         send(place(gx_a, gys[i]), [to_b, mate])
-    arrive(place(gx_ab, gy))
-    send(place(gx_ab, gy), [mate])
-    for i in order[1:]:
-        arrive(place(gx_b, gys[i]))
-        send(place(gx_b, gys[i]), [mate])
-        arrive(place(gx_ab, gys[i]))
-        send(place(gx_ab, gys[i]), [mate])
+
+    def from_b(x, i):
+        arrive(place(x, gys[i]))
+        send(place(x, gys[i]), [mate])
+
+    send(own, [to_a, to_b] + along + [mate])
+    from_a(0)
+    ahead = []
+    for i in order:
+        from_along(i)
+        if ahead:
+            from_a(ahead.pop(0))
+        ahead.append(i)
+    for i in ahead:
+        from_a(i)
+    from_b(gx_b, 0)
+    from_b(gx_ab, 0)
+    for i in order:
+        from_b(gx_b, i)
+        from_b(gx_ab, i)
     for x in (gx, gx_a, gx_b, gx_ab):
         for y in gys:
             arrive(grid_place(x, y, 1 - row, n_gy, n_row))
@@ -268,9 +283,9 @@
     nchunks = packed_ref.shape[0]
 
     def pull(chunk, into):
-        first = chunk * CHUNK
+        names = index_ref.at[pl.ds(chunk * CHUNK, CHUNK)]
         for i in range(CHUNK):
-            into[i:i + 1, :] = wide_ref[pl.ds(index_ref[first + i], 1), :]
+            into[i:i + 1, :] = wide_ref[pl.ds(names[i], 1), :]
 
     def fold(chunk, held):
         packed = packed_ref[pl.ds(chunk, 1), :]
@@ -344,21 +359,22 @@
     sbits = (stripes - 1).bit_length()
     bbits = (nbin - 1).bit_length()
 
-    mine = lax.dynamic_slice_in_dim(columns, lax.axis_index("row") * half, half, 1)
     vmem = pl.BlockSpec(memory_space=pltpu.VMEM)
     sends = n_gy - 1 + 3 + (n_gy - 1) * 3 + n_gy * 2 + n_gy * 2
     table = pl.pallas_call(
         lambda *refs: table_kernel(*refs, npred=npred, stripes=stripes, n_gy=n_gy, n_row=nrow),
         out_shape=jax.ShapeDtypeStruct((total, LANES), jnp.bfloat16),
-        in_specs=[vmem, vmem],
+        in_specs=[vmem, pl.BlockSpec(memory_space=pl.ANY)],
         out_specs=vmem,
         scratch_shapes=[
+            pltpu.VMEM((levels, half), columns.dtype),
+            pltpu.SemaphoreType.DMA,
             pltpu.SemaphoreType.DMA((sends,)),
             pltpu.SemaphoreType.DMA((owners * nrow,)),
         ],
         compiler_params=pltpu.CompilerParams(collective_id=0, has_side_effects=True),
         name="table",
-    )(level_weights, mine)
+    )(level_weights.T, columns)
 
     index = (col_owner[:, 0] * nrow + col_local // half) * rows + col_local % rows
     stripe = (col_local % half) // rows

time: 90.1 us -> 87.5 us (0.971)
  Pallas kernels: 79.6 us -> 77.1 us
  local copies, waits for them, and re-layouts: 9.23 us -> 7.28 us
  other arithmetic: 0.19 us -> 1.93 us
    unnamed x23 -> x6, local copies, waits for them, and re-layouts: 8.09 us -> 5.69 us
    pallas_call x1, Pallas kernels: 33.6 us -> 32.1 us  [local(): pl.pallas_call(lambda *refs: table_kernel(*refs, npred=npred, stripes=str...]
    dynamic_slice x1 -> x0, local copies, waits for them, and re-layouts: 1.09 us -> none  [local(): lax.dynamic_slice_in_dim(columns, lax.axis_index('row') * half, half, 1)]
    or x1, other arithmetic: 0.13 us -> 1.03 us  [local(): packed = stripe | orbit_bin << sbits | group_id << sbits + bbits]
where the time goes in v3:
time: 87.5 us; the launch traced here: 87 us
  Pallas kernels  77.1 us (88%)
  local copies, waits for them, and re-layouts  7.28 us (8%)
  other arithmetic  1.93 us (2%)
    pallas_call x1, Pallas kernels, local(): pl.pallas_call(lambda *refs: table_kernel(*refs, npred=npred, stripes=str...  32.1 us
    pallas_call x1, Pallas kernels, local(): pl.pallas_call(lambda *refs: stats_kernel(*refs, npred=npred, stripes=str...  27.3 us
    pallas_call x1, Pallas kernels, local(): pl.pallas_call(lambda *refs: reduce_kernel(*refs, npred=npred, n_gx=n_gx,...  17.6 us
    unnamed x6, local copies, waits for them, and re-layouts  5.69 us

profile of v3, /device:TPU:0, one launch (start us, length us, event | category | flops | bytes accessed | tf_op | source)
XLA Modules:
  0.0 87.0 jit_solution(3416845718222899399)
XLA Ops:
  0.6 0.7 pad.4.refs_4_
  1.3 0.9 %broadcast_multiply_fusion = s32[16384,1]{0,1:T(1,128)S(1)} fusion(s32[16384,1]{0,1:T(1,128)} %param.11), kind=kLoop, calls=%fused_computation.23 | loop fusion | flops 16384 | bytes 131072 | tf_op jit(solution)/shard_map/mul | solution.py:379
  2.2 0.9 reshape.16.refs_3_
  3.1 1.0 %fusion.5 = (s32[16384]{0:T(1024)S(1)}, s32[16384]{0:T(1024)S(1)}) fusion(s32[16384]{0:T(1024)} %param.14, s32[16384]{0:T(1024)} %param.13, s32[16384]{0:T(1024)} %param.12, s32[16384]{0:T(1024)S(1)} %bitcast.3), kind=kLoop, calls=%fused_computation.16 | loop fusion | flops 802816 | bytes 393216 | tf_op jit(solution)/shard_map/or | solution.py:381
  4.2 32.1 %table.1.refs_1_ = bf16[16384,128]{1,0:T(8,128)(2,1)} custom-call(bf16[16,137]{1,0:T(8,128)(2,1)} %bitcast.5, bf16[137,8192]{1,0:T(8,128)(2,1)} %refs_1_.1), custom_call_target="tpu_custom_call" | custom-call | tf_op jit(solution)/shard_map/table/pallas_call | solution.py:364
  36.3 0.0 copy-start
  36.3 2.2 %copy-done = bf16[16384,128]{1,0:T(8,128)(2,1)S(1)} copy-done((bf16[16384,128]{1,0:T(8,128)(2,1)S(1)}, bf16[16384,128]{1,0:T(8,128)(2,1)}, u32[]{:S(2)}) %copy-start) | copy-done | bytes 4194328
  38.5 27.3 %stats.1.refs_0_ = f32[2,128,128]{2,1,0:T(8,128)S(1)} custom-call(s32[16384]{0:T(1024)S(1)} %get-tuple-element.7.refs_0_, bf16[16384,128]{1,0:T(8,128)(2,1)S(1)} %copy-done, s32[64,256]{1,0:T(8,128)S(1)} %reshape.15.refs_2_, f32[64,256]{1,0:T(8,128)S(1)} %reshape.16.refs_3_, f32[16,128]{1,0:T(8,128)S(1)} %pad.4.refs_4_), custom_call_target="tpu_custom_call" | custom-call | tf_op jit(solution)/shard_map/stats/pallas_call | solution.py:386
  65.8 0.0 copy-start.1
  65.8 0.6 copy-done.1
  66.5 17.6 %reduce.1 = (f32[256,32]{1,0:T(8,128)}, f32[16,32]{1,0:T(8,128)}) custom-call(f32[2,128,128]{2,1,0:T(8,128)} %copy-done.1), custom_call_target="tpu_custom_call" | custom-call | tf_op jit(solution)/shard_map/reduce/pallas_call | solution.py:403
  84.1 1.6 %copy.12 = f32[16,16,32]{2,1,0:T(8,128)} copy(f32[16,16,32]{2,1,0:T(8,128)} %bitcast.4) | data formatting | bytes 65536
  85.7 1.3 %copy.13 = f32[16,32]{1,0:T(8,128)} copy(f32[16,32]{1,0:T(8,128)} %get-tuple-element.11) | data formatting | bytes 4096
  (1 shorter events, 0.0 us)
Async XLA Ops:
  36.3 2.2 %copy-start = (bf16[16384,128]{1,0:T(8,128)(2,1)S(1)}, bf16[16384,128]{1,0:T(8,128)(2,1)}, u32[]{:S(2)}) copy-start(bf16[16384,128]{1,0:T(8,128)(2,1)} %table.1.refs_1_) | copy-start | bytes 12582916
  65.8 0.7 copy-start.1
